TPU v7x, 256 devices: a whole 4x4x8 slice. The times are simulated.
256 devices in a mesh: tm: 64 (over z, x, core), blk: 4 (over y).
Axes of the slice: x: 4, y: 4, z: 8, core: 2. Of those that a mesh axis runs over, the one named last changes fastest.
Arguments:
- prior_mean: float32 [512], replicated, may hold values from -6 to 6
- after_mean: float32 [512], replicated, may hold values from -6 to 6
- filter_map: float32 [128, 512, 512], P('tm', 'blk'), may hold values from -1 to 1.5
- smoother_gain: float32 [128, 512, 512], P('tm', 'blk'), may hold values from -1 to 1.5
- smoother_map: float32 [128, 512, 512], P('tm', 'blk'), may hold values from -1 to 1.5
- obs_gain: float32 [128, 512, 128], P('tm', 'blk'), may hold values from -0.5 to 0.5
- observations: float32 [128, 128], P('tm'), may hold values from -6 to 6
Outputs:
- filtered: float32 [128, 512], P('tm', 'blk')
- smoothed: float32 [128, 512], P('tm', 'blk')
All inputs are finite; a program needn't handle non-finite values.
Results may differ from a plain program's by a relative error of at most 0.0003.
Values sent between devices are 32-bit elements; how exact they have to be, the bound alone decides.
A program may use at most 128 MiB of HBM per device.

v0:
```python
import jax
import jax.numpy as jnp
from jax import lax
from jax.sharding import Mesh
from jax.sharding import PartitionSpec as P

TM = ("tm_0", "tm_1", "tm_2")


def neutral_like(value, identity):
    return jax.tree.map(
        lambda part, zero: jnp.zeros_like(part) + jnp.asarray(zero, part.dtype), value, identity
    )


def prefix_by_axis(value, axes, combine, identity, reverse):
    before = start = neutral_like(value, identity)
    so_far = value
    for axis in reversed(axes):
        length, index = (lax.axis_size(axis), lax.axis_index(axis))
        pieces = jax.tree.map(lambda part: lax.all_gather(part, axis), so_far)
        inside, so_far = (start, start)
        for k in reversed(range(length)) if reverse else range(length):
            passed = k > index if reverse else k < index
            so_far = combine(so_far, jax.tree.map(lambda part: part[k], pieces))
            inside = jax.tree.map(lambda new, old: jnp.where(passed, new, old), so_far, inside)
        before = combine(inside, before)
    return before


def chain_combine(earlier, later):
    highest = lax.Precision.HIGHEST
    joined_map = jnp.dot(later[0], earlier[0], precision=highest)
    joined_offset = jnp.dot(later[0], earlier[1], precision=highest) + later[1]
    return (joined_map, joined_offset)


def shards(prior_mean, after_mean, filter_map, smoother_gain, smoother_map, obs_gain, observations):
    highest = lax.Precision.HIGHEST
    steps = filter_map.shape[0]
    rows = filter_map.shape[1]
    width = filter_map.shape[2]
    first_row = lax.axis_index("blk") * rows
    drive_rows = jnp.einsum("tro,to->tr", obs_gain, observations, precision=highest)
    full_filter, full_gain, drive = (
        lax.all_gather(filter_map, "blk", axis=1, tiled=True),
        lax.all_gather(smoother_gain, "blk", axis=1, tiled=True),
        lax.all_gather(drive_rows, "blk", axis=1, tiled=True),
    )
    identity = jnp.eye(width, dtype=jnp.float32)
    nothing = jnp.zeros((width,), jnp.float32)
    offset = nothing
    for index in range(steps):
        offset = jnp.dot(full_filter[index], offset, precision=highest) + drive[index]
    composite = full_filter[steps - 1]
    index = 0
    composite = jnp.dot(composite, full_filter[index], precision=highest)
    total = prefix_by_axis((composite, offset), TM, chain_combine, (identity, nothing), False)
    entering = jnp.dot(total[0], prior_mean, precision=highest) + total[1]
    current = entering
    filtered_list = []
    for index in range(steps):
        current = jnp.dot(full_filter[index], current, precision=highest) + drive[index]
        filtered_list.append(current)
    filtered_full = jnp.stack(filtered_list, axis=0)
    filtered_rows = lax.dynamic_slice_in_dim(filtered_full, first_row, rows, 1)
    pulled_rows = jnp.einsum("trk,tk->tr", smoother_map, filtered_full, precision=highest)
    pulled = lax.all_gather(pulled_rows, "blk", axis=1, tiled=True)
    offset = nothing
    for index in range(steps - 1, -1, -1):
        offset = jnp.dot(full_gain[index], offset, precision=highest) + pulled[index]
    composite = full_gain[0]
    index = 1
    composite = jnp.dot(composite, full_gain[index], precision=highest)
    total = prefix_by_axis((composite, offset), TM, chain_combine, (identity, nothing), True)
    leaving = jnp.dot(total[0], after_mean, precision=highest) + total[1]
    current = leaving
    smoothed_list = []
    for index in range(steps - 1, -1, -1):
        current = jnp.dot(full_gain[index], current, precision=highest) + pulled[index]
        smoothed_list.append(current)
    smoothed_full = jnp.stack(smoothed_list[::-1], axis=0)
    smoothed_rows = lax.dynamic_slice_in_dim(smoothed_full, first_row, rows, 1)
    return (filtered_rows, smoothed_rows)


def solution(mesh):
    torus = Mesh(mesh.devices.reshape(8, 4, 2, mesh.shape["blk"]), ("tm_0", "tm_1", "tm_2", "blk"))
    in_specs = (
        P(),
        P(),
        P(TM, "blk", None),
        P(TM, "blk", None),
        P(TM, "blk", None),
        P(TM, "blk", None),
        P(TM, None),
    )
    out_specs = (P(TM, "blk"), P(TM, "blk"))
    return jax.shard_map(
        shards, mesh=torus, in_specs=in_specs, out_specs=out_specs, check_vma=False
    )
```

profile of v0, /device:TPU:1, one launch (start us, length us, event | category | flops | bytes accessed | tf_op | source)
XLA Modules:
  0.0 462.8 jit_solution(7283257458123513231)
XLA Ops:
  8.7 38.1 %all-gather.27.cloned.1.call-done = f32[2,512,512]{2,1,0:T(8,128)} async-done(((f32[2,128,512]{2,1,0:T(8,128)}), f32[2,512,512]{2,1,0:T(8,128)}) %all-gather.27.cloned.1.call-update) | async-done | bytes 2097168 | tf_op jit(solution)/shard_map/all_gather | solution.py:46
  46.8 4.4 fusion.142
  51.2 30.8 %all-gather.29.cloned.1.call-done = f32[2,512,512]{2,1,0:T(8,128)} async-done(((f32[2,128,512]{2,1,0:T(8,128)}), f32[2,512,512]{2,1,0:T(8,128)}) %all-gather.29.cloned.1.call-update) | async-done | bytes 2097168 | tf_op jit(solution)/shard_map/all_gather | solution.py:47
  82.0 4.4 fusion.147
  86.5 14.2 %all-gather.31.cloned.1.call-done = f32[1024,512]{1,0:T(8,128)} async-done(((f32[512,512]{1,0:T(8,128)}), f32[1024,512]{1,0:T(8,128)}) %all-gather.31.cloned.1.call-update) | async-done | bytes 2097168 | tf_op jit(solution)/shard_map/all_gather | solution.py:21
  102.9 4.4 fusion.136
  107.4 12.2 %all-gather.37.cloned.1.call-done = f32[1024,512]{1,0:T(8,128)} async-done(((f32[512,512]{1,0:T(8,128)}), f32[1024,512]{1,0:T(8,128)}) %all-gather.37.cloned.1.call-update) | async-done | bytes 2097168 | tf_op jit(solution)/shard_map/all_gather | solution.py:21
  121.8 4.4 fusion.84
  126.4 46.0 %all-gather.33.cloned.1.call-done = f32[2048,512]{1,0:T(8,128)} async-done(((f32[512,512]{1,0:T(8,128)}), f32[2048,512]{1,0:T(8,128)}) %all-gather.33.cloned.1.call-update) | async-done | bytes 4194320 | tf_op jit(solution)/shard_map/all_gather | solution.py:21
  175.8 3.1 fusion.121
  182.7 2.8 fusion.129
  186.0 8.1 %all_gather.91 = f32[2,512]{1,0:T(2,128)S(1)} all-gather(f32[2,128]{1,0:T(2,128)S(1)} %bitcast.347), channel_id=1, replica_groups=mesh['tm_0'=8,'tm_1'=4,'tm_2'=2,'blk'=4] {'blk'}, dimensions={1}, use_global_device_ids=true | all-gather | bytes 5120 | tf_op jit(solution)/shard_map/all_gather | solution.py:48
  198.5 4.2 all-gather.12
  203.6 21.6 %all-gather.39.cloned.1.call-done = f32[2048,512]{1,0:T(8,128)} async-done(((f32[512,512]{1,0:T(8,128)}), f32[2048,512]{1,0:T(8,128)}) %all-gather.39.cloned.1.call-update) | async-done | bytes 4194320 | tf_op jit(solution)/shard_map/all_gather | solution.py:21
  228.5 3.1 fusion.69
  235.5 2.8 fusion.77
  238.4 2.5 fusion.134
  243.2 9.4 %all-gather.13 = f32[4,1,512]{2,1,0:T(1,128)S(1)} all-gather(f32[1,1,512]{2,1,0:T(1,128)S(1)} %bitcast.331), channel_id=6, replica_groups=mesh['tm_0'=8,'tm_1'=4,'tm_2'=2,'blk'=4] {'tm_1'}, dimensions={0}, use_global_device_ids=true | all-gather | bytes 10240 | tf_op jit(solution)/shard_map/all_gather | solution.py:21
  261.7 22.3 %all-gather.14 = f32[8,1,512]{2,1,0:T(1,128)S(1)} all-gather(f32[1,1,512]{2,1,0:T(1,128)S(1)} %bitcast.342), channel_id=7, replica_groups=mesh['tm_0'=8,'tm_1'=4,'tm_2'=2,'blk'=4] {'tm_0'}, dimensions={0}, use_global_device_ids=true | all-gather | bytes 18432 | tf_op jit(solution)/shard_map/all_gather | solution.py:21
  284.0 2.4 fusion.67
  287.4 3.0 fusion.6
  290.4 3.0 fusion.20
  293.4 28.4 %all-gather.35.cloned.1.call-done = f32[4096,512]{1,0:T(8,128)} async-done(((f32[512,512]{1,0:T(8,128)}), f32[4096,512]{1,0:T(8,128)}) %all-gather.35.cloned.1.call-update) | async-done | bytes 8388624 | tf_op jit(solution)/shard_map/all_gather | solution.py:21
  324.1 2.3 fusion.93
  326.5 2.5 fusion.97
  361.3 8.5 %all_gather.105 = f32[2,512]{1,0:T(2,128)S(1)} all-gather(f32[2,128]{1,0:T(2,128)S(1)} %bitcast.346), channel_id=1, replica_groups=mesh['tm_0'=8,'tm_1'=4,'tm_2'=2,'blk'=4] {'blk'}, dimensions={1}, use_global_device_ids=true | all-gather | bytes 5120 | tf_op jit(solution)/shard_map/all_gather | solution.py:68
  370.8 3.6 all-gather.15
  375.4 9.5 %all-gather.16 = f32[4,1,512]{2,1,0:T(1,128)S(1)} all-gather(f32[1,1,512]{2,1,0:T(1,128)S(1)} %bitcast.330), channel_id=12, replica_groups=mesh['tm_0'=8,'tm_1'=4,'tm_2'=2,'blk'=4] {'tm_1'}, dimensions={0}, use_global_device_ids=true | all-gather | bytes 10240 | tf_op jit(solution)/shard_map/all_gather | solution.py:21
  387.9 19.5 %all-gather.17 = f32[8,1,512]{2,1,0:T(1,128)S(1)} all-gather(f32[1,1,512]{2,1,0:T(1,128)S(1)} %bitcast.339), channel_id=13, replica_groups=mesh['tm_0'=8,'tm_1'=4,'tm_2'=2,'blk'=4] {'tm_0'}, dimensions={0}, use_global_device_ids=true | all-gather | bytes 18432 | tf_op jit(solution)/shard_map/all_gather | solution.py:21
  408.7 7.8 %all-gather.41.cloned.1.call-done = f32[4096,512]{1,0:T(8,128)} async-done(((f32[512,512]{1,0:T(8,128)}), f32[4096,512]{1,0:T(8,128)}) %all-gather.41.cloned.1.call-update) | async-done | bytes 8388624 | tf_op jit(solution)/shard_map/all_gather | solution.py:21
  418.8 2.3 fusion.41
  421.2 2.5 fusion.45
  (206 shorter events, 113.7 us)
Async XLA Ops:
  7.2 353.7 %copy-start = (f32[2,128,512]{2,1,0:T(8,128)S(1)}, f32[2,128,512]{2,1,0:T(8,128)}, u32[]{:S(2)}) copy-start(f32[2,128,512]{2,1,0:T(8,128)} %param.11) | copy-start | bytes 1572868
  7.2 39.6 %all-gather.27.cloned.1.call-start = ((), (), s32[]{:S(2)}) async-start(), calls=%async_computation | async-start | bytes 2621440 | tf_op jit(solution)/shard_map/all_gather | solution.py:46
  7.9 74.1 %all-gather.29.cloned.1.call-start = ((), (), s32[]{:S(2)}) async-start(), calls=%async_computation.1 | async-start | bytes 2621440 | tf_op jit(solution)/shard_map/all_gather | solution.py:47
  8.7 92.0 %all-gather.31.cloned.1.call-start = ((), (), s32[]{:S(2)}) async-start(), calls=%async_computation.2 | async-start | bytes 3145728 | tf_op jit(solution)/shard_map/all_gather | solution.py:21
  51.2 68.4 %all-gather.37.cloned.1.call-start = ((), (), s32[]{:S(2)}) async-start(), calls=%async_computation.5 | async-start | bytes 3145728 | tf_op jit(solution)/shard_map/all_gather | solution.py:21
  86.4 86.0 %all-gather.33.cloned.1.call-start = ((), (), s32[]{:S(2)}) async-start(), calls=%async_computation.3 | async-start | bytes 5242880 | tf_op jit(solution)/shard_map/all_gather | solution.py:21
  102.9 23.3 %copy-start.13 = (f32[512,512]{1,0:T(8,128)}, f32[512,512]{1,0:T(8,128)S(1)}, u32[]{:S(2)}) copy-start(f32[512,512]{1,0:T(8,128)S(1)} %fusion.35) | copy-start | bytes 3145732
  107.3 117.9 %all-gather.39.cloned.1.call-start = ((), (), s32[]{:S(2)}) async-start(), calls=%async_computation.6 | async-start | bytes 5242880 | tf_op jit(solution)/shard_map/all_gather | solution.py:21
  121.8 53.0 %copy-start.16 = (f32[512,512]{1,0:T(8,128)}, f32[512,512]{1,0:T(8,128)S(1)}, u32[]{:S(2)}) copy-start(f32[512,512]{1,0:T(8,128)S(1)} %fusion.31) | copy-start | bytes 3145732
  126.2 195.6 %all-gather.35.cloned.1.call-start = ((), (), s32[]{:S(2)}) async-start(), calls=%async_computation.4 | async-start | bytes 9437184 | tf_op jit(solution)/shard_map/all_gather | solution.py:21
  172.4 7.4 %copy-start.7 = (f32[2048,512]{1,0:T(8,128)S(1)}, f32[2048,512]{1,0:T(8,128)}, u32[]{:S(2)}) copy-start(f32[2048,512]{1,0:T(8,128)} %all-gather.33.cloned.1.call-done) | copy-start | bytes 12582916
  179.8 22.9 %copy-start.3 = (f32[2,512,512]{2,1,0:T(8,128)S(1)}, f32[2,512,512]{2,1,0:T(8,128)}, u32[]{:S(2)}) copy-start(f32[2,512,512]{2,1,0:T(8,128)} %all-gather.29.cloned.1.call-done) | copy-start | bytes 6291460
  185.6 231.0 %all-gather.41.cloned.1.call-start = ((), (), s32[]{:S(2)}) async-start(), calls=%async_computation.7 | async-start | bytes 9437184 | tf_op jit(solution)/shard_map/all_gather | solution.py:21
  225.2 7.4 %copy-start.5 = (f32[2048,512]{1,0:T(8,128)S(1)}, f32[2048,512]{1,0:T(8,128)}, u32[]{:S(2)}) copy-start(f32[2048,512]{1,0:T(8,128)} %all-gather.39.cloned.1.call-done) | copy-start | bytes 12582916
  238.3 16.9 %copy-start.14 = (f32[512,512]{1,0:T(8,128)S(1)}, f32[512,512]{1,0:T(8,128)}, u32[]{:S(2)}) copy-start(f32[512,512]{1,0:T(8,128)} %copy-done.13) | copy-start | bytes 3145732
  238.3 16.9 %copy-start.15 = (f32[512,512]{1,0:T(8,128)S(1)}, f32[512,512]{1,0:T(8,128)}, u32[]{:S(2)}) copy-start(f32[512,512]{1,0:T(8,128)} %fusion.136) | copy-start | bytes 3145732
  238.3 18.1 %copy-start.17 = (f32[512,512]{1,0:T(8,128)S(1)}, f32[512,512]{1,0:T(8,128)}, u32[]{:S(2)}) copy-start(f32[512,512]{1,0:T(8,128)} %copy-done.16) | copy-start | bytes 3145732
  238.3 18.1 %copy-start.18 = (f32[512,512]{1,0:T(8,128)S(1)}, f32[512,512]{1,0:T(8,128)}, u32[]{:S(2)}) copy-start(f32[512,512]{1,0:T(8,128)} %fusion.84) | copy-start | bytes 3145732
  240.8 16.8 %copy-start.8 = (f32[2048,512]{1,0:T(8,128)S(1)}, f32[2048,512]{1,0:T(8,128)}, u32[]{:S(2)}) copy-start(f32[2048,512]{1,0:T(8,128)} %all-gather.33.cloned.1.call-done) | copy-start | bytes 12582916
  256.4 31.0 %copy-start.10 = (f32[512,512]{1,0:T(8,128)S(1)}, f32[512,512]{1,0:T(8,128)}, u32[]{:S(2)}) copy-start(f32[512,512]{1,0:T(8,128)} %copy-done.9) | copy-start | bytes 3145732
  256.4 31.0 %copy-start.12 = (f32[512,512]{1,0:T(8,128)S(1)}, f32[512,512]{1,0:T(8,128)}, u32[]{:S(2)}) copy-start(f32[512,512]{1,0:T(8,128)} %copy-done.11) | copy-start | bytes 3145732
  256.4 31.0 %copy-start.25 = (f32[512,512]{1,0:T(8,128)S(1)}, f32[512,512]{1,0:T(8,128)}, u32[]{:S(2)}) copy-start(f32[512,512]{1,0:T(8,128)} %fusion.129) | copy-start | bytes 3145732
  256.4 31.0 %copy-start.27 = (f32[512,512]{1,0:T(8,128)S(1)}, f32[512,512]{1,0:T(8,128)}, u32[]{:S(2)}) copy-start(f32[512,512]{1,0:T(8,128)} %copy-done.26) | copy-start | bytes 3145732
  257.6 32.8 %copy-start.31 = (f32[512,512]{1,0:T(8,128)}, f32[512,512]{1,0:T(8,128)S(1)}, u32[]{:S(2)}) copy-start(f32[512,512]{1,0:T(8,128)S(1)} %fusion.15) | copy-start | bytes 3145732
  284.0 6.4 %copy-start.22 = (f32[512,512]{1,0:T(8,128)S(1)}, f32[512,512]{1,0:T(8,128)}, u32[]{:S(2)}) copy-start(f32[512,512]{1,0:T(8,128)} %copy-done.21) | copy-start | bytes 3145732
  321.8 18.5 %copy-start.30 = (f32[512,512]{1,0:T(8,128)S(1)}, f32[512,512]{1,0:T(8,128)}, u32[]{:S(2)}) copy-start(f32[512,512]{1,0:T(8,128)} %fusion.6) | copy-start | bytes 3145732
  324.1 17.1 %copy-start.2 = (f32[4096,512]{1,0:T(8,128)S(1)}, f32[4096,512]{1,0:T(8,128)}, u32[]{:S(2)}) copy-start(f32[4096,512]{1,0:T(8,128)} %all-gather.35.cloned.1.call-done) | copy-start | bytes 25165828
  353.6 20.8 %copy-start.33 = (f32[1024,512]{1,0:T(8,128)S(1)}, f32[1024,512]{1,0:T(8,128)}, u32[]{:S(2)}) copy-start(f32[1024,512]{1,0:T(8,128)} %all-gather.37.cloned.1.call-done) | copy-start | bytes 6291460
  355.9 28.9 %copy-start.6 = (f32[2048,512]{1,0:T(8,128)S(1)}, f32[2048,512]{1,0:T(8,128)}, u32[]{:S(2)}) copy-start(f32[2048,512]{1,0:T(8,128)} %all-gather.39.cloned.1.call-done) | copy-start | bytes 12582916
  358.8 48.9 %copy-start.32 = (f32[512,512]{1,0:T(8,128)S(1)}, f32[512,512]{1,0:T(8,128)}, u32[]{:S(2)}) copy-start(f32[512,512]{1,0:T(8,128)} %copy-done.31) | copy-start | bytes 3145732
  416.5 18.3 %copy-start.24 = (f32[512,512]{1,0:T(8,128)S(1)}, f32[512,512]{1,0:T(8,128)}, u32[]{:S(2)}) copy-start(f32[512,512]{1,0:T(8,128)} %fusion.20) | copy-start | bytes 3145732
  418.8 17.0 %copy-start.1 = (f32[4096,512]{1,0:T(8,128)S(1)}, f32[4096,512]{1,0:T(8,128)}, u32[]{:S(2)}) copy-start(f32[4096,512]{1,0:T(8,128)} %all-gather.41.cloned.1.call-done) | copy-start | bytes 25165828
  (14 other events, 48.1 us)
Sparse Core Ops, SparseCore 0:
  9.8 36.9 all-gather.26
  48.6 33.3 all-gather.28
  83.8 16.8 all-gather.30
  102.3 17.1 all-gather.36
  121.2 51.1 all-gather.32
  174.1 51.0 all-gather.38
  227.0 94.7 all-gather.34
  323.6 92.9 all-gather.40
where the time goes:
time: 471 us; the launch traced here: 463 us
  waiting for transfers between devices  200 us (42%)
  matrix products  155 us (33%)
  blocking collectives  85.1 us (18%)
  between operations  15.1 us (3%)
  local copies, waits for them, and re-layouts  6.15 us (1%)
    all_gather x6, waiting for transfers between devices, prefix_by_axis(): pieces = jax.tree.map(lambda part: lax.all_gather(part, axis), so_far)  130 us
    dot_general x34, matrix products, chain_combine(): joined_map = jnp.dot(later[0], earlier[0], precision=highest)  74.4 us
    all_gather x6, blocking collectives, prefix_by_axis(): pieces = jax.tree.map(lambda part: lax.all_gather(part, axis), so_far)  68.5 us
    dot_general x34, matrix products, chain_combine(): joined_offset = jnp.dot(later[0], earlier[1], precision=highest) + later[1]  58.5 us
    all_gather x1, waiting for transfers between devices, shards(): lax.all_gather(filter_map, 'blk', axis=1, tiled=True)  38.1 us
    all_gather x1, waiting for transfers between devices, shards(): lax.all_gather(smoother_gain, 'blk', axis=1, tiled=True)  30.8 us
  transfers between devices with their start and end apart: 8, of which 8 were waited for; matrix products, arithmetic and copies ran while one was open for 25% of the time, Pallas kernels for 0%

commit v1 on v0

--- a/solution.py
+++ b/solution.py
@@ -43,7 +43,12 @@
     first_row = lax.axis_index("blk") * rows
     drive_rows = jnp.einsum("tro,to->tr", obs_gain, observations, precision=highest)
     full_filter, full_gain, drive = (
-        lax.all_gather(filter_map, "blk", axis=1, tiled=True),
+        jnp.concatenate(
+            lax.all_to_all(
+                jnp.stack([filter_map for _ in range(lax.axis_size("blk"))]), "blk", 0, 0
+            ),
+            axis=1,
+        ),
         lax.all_gather(smoother_gain, "blk", axis=1, tiled=True),
         lax.all_gather(drive_rows, "blk", axis=1, tiled=True),
     )

time: 471 us -> 448 us (0.951)
  waiting for transfers between devices: 200 us -> 140 us
  blocking collectives: 85.1 us -> 125 us
  matrix products: 155 us -> 149 us
    all_to_all x0 -> x1, blocking collectives: none -> 39.5 us  [shards(): lax.all_to_all(jnp.stack([filter_map for _ in range(lax.axis_size('blk'))...]
    all_gather x1 -> x0, waiting for transfers between devices: 38.1 us -> none  [shards(): lax.all_gather(filter_map, 'blk', axis=1, tiled=True)]
    all_gather x1, waiting for transfers between devices: 30.8 us -> 5.87 us  [shards(): lax.all_gather(smoother_gain, 'blk', axis=1, tiled=True)]
  transfers between devices with their start and end apart: 8 -> 7, of which waited for: 8 -> 7; matrix products, arithmetic and copies ran while one was open for 25% -> 26% of each run, Pallas kernels for 0% -> 0%
where the time goes in v1:
time: 448 us; the launch traced here: 439 us
  matrix products  149 us (33%)
  waiting for transfers between devices  140 us (31%)
  blocking collectives  125 us (28%)
  between operations  15.2 us (3%)
  local copies, waits for them, and re-layouts  9.67 us (2%)
    all_gather x6, waiting for transfers between devices, prefix_by_axis(): pieces = jax.tree.map(lambda part: lax.all_gather(part, axis), so_far)  133 us
    dot_general x34, matrix products, chain_combine(): joined_map = jnp.dot(later[0], earlier[0], precision=highest)  73.7 us
    all_gather x6, blocking collectives, prefix_by_axis(): pieces = jax.tree.map(lambda part: lax.all_gather(part, axis), so_far)  68.5 us
    dot_general x34, matrix products, chain_combine(): joined_offset = jnp.dot(later[0], earlier[1], precision=highest) + later[1]  57.7 us
    all_to_all x1, blocking collectives, shards(): lax.all_to_all(jnp.stack([filter_map for _ in range(lax.axis_size('blk'))...  39.5 us
  transfers between devices with their start and end apart: 7, of which 7 were waited for; matrix products, arithmetic and copies ran while one was open for 26% of the time, Pallas kernels for 0%

profile of v1, /device:TPU:1, one launch (start us, length us, event | category | flops | bytes accessed | tf_op | source)
XLA Modules:
  0.0 439.4 jit_solution(847145064382921883)
XLA Ops:
  9.3 39.5 %all_to_all.5 = f32[4,2,128,512]{3,2,1,0:T(8,128)S(1)} all-to-all(f32[4,2,128,512]{3,2,1,0:T(8,128)S(1)} %stack.25), channel_id=1, replica_groups=mesh['tm_0'=8,'tm_1'=4,'tm_2'=2,'blk'=4] {'blk'}, dimensions={0} | all-to-all | bytes 4194304 | tf_op jit(solution)/shard_map/all_to_all | solution.py:47
  48.9 2.9 fusion.188
  51.9 5.9 %all-gather.26.cloned.1.call-done = f32[2,512,512]{2,1,0:T(8,128)} async-done(((f32[2,128,512]{2,1,0:T(8,128)}), f32[2,512,512]{2,1,0:T(8,128)}) %all-gather.26.cloned.1.call-update) | async-done | bytes 2097168 | tf_op jit(solution)/shard_map/all_gather | solution.py:52
  57.7 4.4 fusion.142
  62.2 15.1 %all-gather.28.cloned.1.call-done = f32[1024,512]{1,0:T(8,128)} async-done(((f32[512,512]{1,0:T(8,128)}), f32[1024,512]{1,0:T(8,128)}) %all-gather.28.cloned.1.call-update) | async-done | bytes 2097168 | tf_op jit(solution)/shard_map/all_gather | solution.py:21
  80.5 4.0 fusion.136
  84.6 11.8 %all-gather.34.cloned.1.call-done = f32[1024,512]{1,0:T(8,128)} async-done(((f32[512,512]{1,0:T(8,128)}), f32[1024,512]{1,0:T(8,128)}) %all-gather.34.cloned.1.call-update) | async-done | bytes 2097168 | tf_op jit(solution)/shard_map/all_gather | solution.py:21
  99.5 4.1 fusion.84
  103.8 45.3 %all-gather.30.cloned.1.call-done = f32[2048,512]{1,0:T(8,128)} async-done(((f32[512,512]{1,0:T(8,128)}), f32[2048,512]{1,0:T(8,128)}) %all-gather.30.cloned.1.call-update) | async-done | bytes 4194320 | tf_op jit(solution)/shard_map/all_gather | solution.py:21
  152.5 3.1 fusion.121
  159.5 2.8 fusion.129
  162.8 8.1 %all_gather.87 = f32[2,512]{1,0:T(2,128)S(1)} all-gather(f32[2,128]{1,0:T(2,128)S(1)} %bitcast.353), channel_id=1, replica_groups=mesh['tm_0'=8,'tm_1'=4,'tm_2'=2,'blk'=4] {'blk'}, dimensions={1}, use_global_device_ids=true | all-gather | bytes 5120 | tf_op jit(solution)/shard_map/all_gather | solution.py:53
  172.8 4.2 all-gather.12
  177.0 25.0 %all-gather.36.cloned.1.call-done = f32[2048,512]{1,0:T(8,128)} async-done(((f32[512,512]{1,0:T(8,128)}), f32[2048,512]{1,0:T(8,128)}) %all-gather.36.cloned.1.call-update) | async-done | bytes 4194320 | tf_op jit(solution)/shard_map/all_gather | solution.py:21
  205.3 3.1 fusion.69
  212.2 2.9 fusion.77
  216.1 3.0 fusion.134
  219.1 2.3 fusion.138
  221.5 9.4 %all-gather.13 = f32[4,1,512]{2,1,0:T(1,128)S(1)} all-gather(f32[1,1,512]{2,1,0:T(1,128)S(1)} %bitcast.338), channel_id=6, replica_groups=mesh['tm_0'=8,'tm_1'=4,'tm_2'=2,'blk'=4] {'tm_1'}, dimensions={0}, use_global_device_ids=true | all-gather | bytes 10240 | tf_op jit(solution)/shard_map/all_gather | solution.py:21
  238.7 22.4 %all-gather.14 = f32[8,1,512]{2,1,0:T(1,128)S(1)} all-gather(f32[1,1,512]{2,1,0:T(1,128)S(1)} %bitcast.348), channel_id=7, replica_groups=mesh['tm_0'=8,'tm_1'=4,'tm_2'=2,'blk'=4] {'tm_0'}, dimensions={0}, use_global_device_ids=true | all-gather | bytes 18432 | tf_op jit(solution)/shard_map/all_gather | solution.py:21
  262.1 3.0 fusion.6
  267.4 3.0 fusion.20
  270.4 28.0 %all-gather.32.cloned.1.call-done = f32[4096,512]{1,0:T(8,128)} async-done(((f32[512,512]{1,0:T(8,128)}), f32[4096,512]{1,0:T(8,128)}) %all-gather.32.cloned.1.call-update) | async-done | bytes 8388624 | tf_op jit(solution)/shard_map/all_gather | solution.py:21
  300.7 2.3 fusion.93
  303.1 2.5 fusion.97
  338.0 8.5 %all_gather.101 = f32[2,512]{1,0:T(2,128)S(1)} all-gather(f32[2,128]{1,0:T(2,128)S(1)} %bitcast.352), channel_id=1, replica_groups=mesh['tm_0'=8,'tm_1'=4,'tm_2'=2,'blk'=4] {'blk'}, dimensions={1}, use_global_device_ids=true | all-gather | bytes 5120 | tf_op jit(solution)/shard_map/all_gather | solution.py:73
  347.5 3.6 all-gather.15
  352.0 9.5 %all-gather.16 = f32[4,1,512]{2,1,0:T(1,128)S(1)} all-gather(f32[1,1,512]{2,1,0:T(1,128)S(1)} %bitcast.337), channel_id=12, replica_groups=mesh['tm_0'=8,'tm_1'=4,'tm_2'=2,'blk'=4] {'tm_1'}, dimensions={0}, use_global_device_ids=true | all-gather | bytes 10240 | tf_op jit(solution)/shard_map/all_gather | solution.py:21
  364.5 19.5 %all-gather.17 = f32[8,1,512]{2,1,0:T(1,128)S(1)} all-gather(f32[1,1,512]{2,1,0:T(1,128)S(1)} %bitcast.346), channel_id=13, replica_groups=mesh['tm_0'=8,'tm_1'=4,'tm_2'=2,'blk'=4] {'tm_0'}, dimensions={0}, use_global_device_ids=true | all-gather | bytes 18432 | tf_op jit(solution)/shard_map/all_gather | solution.py:21
  385.4 7.8 %all-gather.38.cloned.1.call-done = f32[4096,512]{1,0:T(8,128)} async-done(((f32[512,512]{1,0:T(8,128)}), f32[4096,512]{1,0:T(8,128)}) %all-gather.38.cloned.1.call-update) | async-done | bytes 8388624 | tf_op jit(solution)/shard_map/all_gather | solution.py:21
  395.4 2.3 fusion.41
  397.8 2.5 fusion.45
  (214 shorter events, 112.7 us)
Async XLA Ops:
  7.2 330.3 %copy-start = (f32[2,128,512]{2,1,0:T(8,128)S(1)}, f32[2,128,512]{2,1,0:T(8,128)}, u32[]{:S(2)}) copy-start(f32[2,128,512]{2,1,0:T(8,128)} %param.11) | copy-start | bytes 1572868
  7.2 50.5 %all-gather.26.cloned.1.call-start = ((), (), s32[]{:S(2)}) async-start(), calls=%async_computation.1 | async-start | bytes 2621440 | tf_op jit(solution)/shard_map/all_gather | solution.py:52
  7.9 69.4 %all-gather.28.cloned.1.call-start = ((), (), s32[]{:S(2)}) async-start(), calls=%async_computation.2 | async-start | bytes 3145728 | tf_op jit(solution)/shard_map/all_gather | solution.py:21
  48.9 122.0 %copy-start.10 = (f32[1,4,128,512]{3,2,0,1:T(8,128)}, f32[1,4,128,512]{3,2,0,1:T(8,128)S(1)}, u32[]{:S(2)}) copy-start(f32[1,4,128,512]{3,2,0,1:T(8,128)S(1)} %get-tuple-element.10) | copy-start | bytes 3145732
  48.9 122.9 %copy-start.8 = (f32[1,4,128,512]{3,2,0,1:T(8,128)}, f32[1,4,128,512]{3,2,0,1:T(8,128)S(1)}, u32[]{:S(2)}) copy-start(f32[1,4,128,512]{3,2,0,1:T(8,128)S(1)} %get-tuple-element.11) | copy-start | bytes 3145732
  51.8 44.5 %all-gather.34.cloned.1.call-start = ((), (), s32[]{:S(2)}) async-start(), calls=%async_computation.5 | async-start | bytes 3145728 | tf_op jit(solution)/shard_map/all_gather | solution.py:21
  62.1 87.0 %all-gather.30.cloned.1.call-start = ((), (), s32[]{:S(2)}) async-start(), calls=%async_computation.3 | async-start | bytes 5242880 | tf_op jit(solution)/shard_map/all_gather | solution.py:21
  84.5 117.4 %all-gather.36.cloned.1.call-start = ((), (), s32[]{:S(2)}) async-start(), calls=%async_computation.6 | async-start | bytes 5242880 | tf_op jit(solution)/shard_map/all_gather | solution.py:21
  103.6 194.8 %all-gather.32.cloned.1.call-start = ((), (), s32[]{:S(2)}) async-start(), calls=%async_computation.4 | async-start | bytes 9437184 | tf_op jit(solution)/shard_map/all_gather | solution.py:21
  149.2 7.4 %copy-start.6 = (f32[2048,512]{1,0:T(8,128)S(1)}, f32[2048,512]{1,0:T(8,128)}, u32[]{:S(2)}) copy-start(f32[2048,512]{1,0:T(8,128)} %all-gather.30.cloned.1.call-done) | copy-start | bytes 12582916
  162.3 230.8 %all-gather.38.cloned.1.call-start = ((), (), s32[]{:S(2)}) async-start(), calls=%async_computation.7 | async-start | bytes 9437184 | tf_op jit(solution)/shard_map/all_gather | solution.py:21
  201.9 7.4 %copy-start.4 = (f32[2048,512]{1,0:T(8,128)S(1)}, f32[2048,512]{1,0:T(8,128)}, u32[]{:S(2)}) copy-start(f32[2048,512]{1,0:T(8,128)} %all-gather.36.cloned.1.call-done) | copy-start | bytes 12582916
  215.1 16.2 %copy-start.17 = (f32[512,512]{1,0:T(8,128)S(1)}, f32[512,512]{1,0:T(8,128)}, u32[]{:S(2)}) copy-start(f32[512,512]{1,0:T(8,128)} %copy-done.16) | copy-start | bytes 3145732
  215.1 16.2 %copy-start.18 = (f32[512,512]{1,0:T(8,128)S(1)}, f32[512,512]{1,0:T(8,128)}, u32[]{:S(2)}) copy-start(f32[512,512]{1,0:T(8,128)} %fusion.136) | copy-start | bytes 3145732
  215.1 17.3 %copy-start.36 = (f32[1024,512]{1,0:T(8,128)S(1)}, f32[1024,512]{1,0:T(8,128)}, u32[]{:S(2)}) copy-start(f32[1024,512]{1,0:T(8,128)} %all-gather.34.cloned.1.call-done) | copy-start | bytes 6291460
  215.1 18.3 %copy-start.20 = (f32[512,512]{1,0:T(8,128)S(1)}, f32[512,512]{1,0:T(8,128)}, u32[]{:S(2)}) copy-start(f32[512,512]{1,0:T(8,128)} %copy-done.19) | copy-start | bytes 3145732
  215.1 18.3 %copy-start.21 = (f32[512,512]{1,0:T(8,128)S(1)}, f32[512,512]{1,0:T(8,128)}, u32[]{:S(2)}) copy-start(f32[512,512]{1,0:T(8,128)} %fusion.84) | copy-start | bytes 3145732
  219.1 15.6 %copy-start.7 = (f32[2048,512]{1,0:T(8,128)S(1)}, f32[2048,512]{1,0:T(8,128)}, u32[]{:S(2)}) copy-start(f32[2048,512]{1,0:T(8,128)} %all-gather.30.cloned.1.call-done) | copy-start | bytes 12582916
  233.4 28.7 %copy-start.13 = (f32[512,512]{1,0:T(8,128)S(1)}, f32[512,512]{1,0:T(8,128)}, u32[]{:S(2)}) copy-start(f32[512,512]{1,0:T(8,128)} %copy-done.12) | copy-start | bytes 3145732
  233.5 28.7 %copy-start.15 = (f32[512,512]{1,0:T(8,128)S(1)}, f32[512,512]{1,0:T(8,128)}, u32[]{:S(2)}) copy-start(f32[512,512]{1,0:T(8,128)} %copy-done.14) | copy-start | bytes 3145732
  233.5 28.7 %copy-start.28 = (f32[512,512]{1,0:T(8,128)S(1)}, f32[512,512]{1,0:T(8,128)}, u32[]{:S(2)}) copy-start(f32[512,512]{1,0:T(8,128)} %fusion.129) | copy-start | bytes 3145732
  233.5 28.7 %copy-start.30 = (f32[512,512]{1,0:T(8,128)S(1)}, f32[512,512]{1,0:T(8,128)}, u32[]{:S(2)}) copy-start(f32[512,512]{1,0:T(8,128)} %copy-done.29) | copy-start | bytes 3145732
  234.7 32.7 %copy-start.34 = (f32[512,512]{1,0:T(8,128)}, f32[512,512]{1,0:T(8,128)S(1)}, u32[]{:S(2)}) copy-start(f32[512,512]{1,0:T(8,128)S(1)} %fusion.15) | copy-start | bytes 3145732
  261.1 6.3 %copy-start.26 = (f32[512,512]{1,0:T(8,128)S(1)}, f32[512,512]{1,0:T(8,128)}, u32[]{:S(2)}) copy-start(f32[512,512]{1,0:T(8,128)} %fusion.77) | copy-start | bytes 3145732
  261.1 6.3 %copy-start.32 = (f32[512,512]{1,0:T(8,128)S(1)}, f32[512,512]{1,0:T(8,128)}, u32[]{:S(2)}) copy-start(f32[512,512]{1,0:T(8,128)} %copy-done.31) | copy-start | bytes 3145732
  298.4 18.5 %copy-start.33 = (f32[512,512]{1,0:T(8,128)S(1)}, f32[512,512]{1,0:T(8,128)}, u32[]{:S(2)}) copy-start(f32[512,512]{1,0:T(8,128)} %fusion.6) | copy-start | bytes 3145732
  300.7 17.1 %copy-start.2 = (f32[4096,512]{1,0:T(8,128)S(1)}, f32[4096,512]{1,0:T(8,128)}, u32[]{:S(2)}) copy-start(f32[4096,512]{1,0:T(8,128)} %all-gather.32.cloned.1.call-done) | copy-start | bytes 25165828
  332.6 18.5 %copy-start.37 = (f32[1024,512]{1,0:T(8,128)S(1)}, f32[1024,512]{1,0:T(8,128)}, u32[]{:S(2)}) copy-start(f32[1024,512]{1,0:T(8,128)} %all-gather.34.cloned.1.call-done) | copy-start | bytes 6291460
  332.6 29.0 %copy-start.5 = (f32[2048,512]{1,0:T(8,128)S(1)}, f32[2048,512]{1,0:T(8,128)}, u32[]{:S(2)}) copy-start(f32[2048,512]{1,0:T(8,128)} %all-gather.36.cloned.1.call-done) | copy-start | bytes 12582916
  335.5 48.9 %copy-start.35 = (f32[512,512]{1,0:T(8,128)S(1)}, f32[512,512]{1,0:T(8,128)}, u32[]{:S(2)}) copy-start(f32[512,512]{1,0:T(8,128)} %copy-done.34) | copy-start | bytes 3145732
  393.1 18.3 %copy-start.27 = (f32[512,512]{1,0:T(8,128)S(1)}, f32[512,512]{1,0:T(8,128)}, u32[]{:S(2)}) copy-start(f32[512,512]{1,0:T(8,128)} %fusion.20) | copy-start | bytes 3145732
  395.4 17.0 %copy-start.1 = (f32[4096,512]{1,0:T(8,128)S(1)}, f32[4096,512]{1,0:T(8,128)}, u32[]{:S(2)}) copy-start(f32[4096,512]{1,0:T(8,128)} %all-gather.38.cloned.1.call-done) | copy-start | bytes 25165828
  (17 other events, 55.4 us)
Sparse Core Ops, SparseCore 0:
  9.8 47.8 all-gather.25
  59.5 17.7 all-gather.27
  79.1 17.1 all-gather.33
  98.0 51.1 all-gather.29
  150.8 51.0 all-gather.35
  203.6 94.7 all-gather.31
  300.2 92.9 all-gather.37
